TPU v7x, 32 devices: a whole 2x2x4 slice. The times are simulated.
32 devices in a mesh: gx: 2 (over x), gy: 4 (over z), gz: 4 (over y, core).
Axes of the slice: x: 2, y: 2, z: 4, core: 2. Of those that a mesh axis runs over, the one named last changes fastest.
Arguments:
- right_side: float32 [16, 64, 512], P('gx', 'gy', 'gz'), may hold values from -40 to 40
- fiber_class: int32 [16, 64, 512], P('gx', 'gy', 'gz'), may hold values from 0 to 15
- conductivity_scale: float32 [16, 64, 512], P('gx', 'gy', 'gz'), may hold values from 0.8 to 1.25
- class_tensor: float32 [6, 16], replicated, may hold values from -0.15 to 1.8, as said below
- block_ids: int32 [2, 4, 8], replicated, may hold values from 0 to 63, as said below
Outputs:
- solution: float32 [16, 64, 512], P('gx', 'gy', 'gz')
- residual: float32 [16, 64, 512], P('gx', 'gy', 'gz')
Inputs may be any that keep to these rules, and one draw needn't show every extreme that they name: `class_tensor`: column k is the tensor t I + (l - t) f f^T for a unit vector f, with 1 <= t <= 1.5 and 1.05 <= l / t <= 1.2. `block_ids`: each subdomain number names exactly 1 block.
All inputs are finite; a program needn't handle non-finite values.
Results may differ from a plain program's by a relative error of at most 0.0003.
Values sent between devices are 32-bit elements; how exact they have to be, the bound alone decides.
A program may use at most 64 MiB of HBM per device.

v0:
```python
import jax
import jax.numpy as jnp
from jax import lax
from jax.sharding import PartitionSpec as P

CX = 8
CY = 16
CZ = 128
ZBLK = 2
BZ = 64
COARSE = 64
NCLS = 16
ITERS = 2


STENCIL_TAPS = (
    (1, 0, 0, 0, 1.0),
    (-1, 0, 0, 0, 1.0),
    (0, 1, 0, 1, 1.0),
    (0, -1, 0, 1, 1.0),
    (0, 0, 1, 2, 1.0),
    (0, 0, -1, 2, 1.0),
    (1, 1, 0, 3, 0.5),
    (-1, -1, 0, 3, 0.5),
    (1, -1, 0, 3, -0.5),
    (-1, 1, 0, 3, -0.5),
    (1, 0, 1, 4, 0.5),
    (-1, 0, -1, 4, 0.5),
    (1, 0, -1, 4, -0.5),
    (-1, 0, 1, 4, -0.5),
    (0, 1, 1, 5, 0.5),
    (0, -1, -1, 5, 0.5),
    (0, 1, -1, 5, -0.5),
    (0, -1, 1, 5, -0.5),
)


def padded_2(cells, sides, width):
    for axis, dim in sides:
        count = lax.axis_size(axis)
        ends = count - 1
        head = lax.slice_in_dim(cells, 0, width, axis=dim)
        tail = lax.slice_in_dim(cells, cells.shape[dim] - width, cells.shape[dim], axis=dim)
        cells = jnp.concatenate(
            [
                lax.ppermute(tail, axis, [(i, (i + 1) % count) for i in range(ends)]),
                cells,
                lax.ppermute(head, axis, [((i + 1) % count, i) for i in range(ends)]),
            ],
            axis=dim,
        )
    return cells


def shifted(padded, step_x, step_y, step_z):
    width_x = padded.shape[-3] - 2
    width_y = padded.shape[-2] - 2
    width_z = padded.shape[-1] - 2
    return padded[
        1 + step_x : 1 + step_x + width_x,
        1 + step_y : 1 + step_y + width_y,
        1 + step_z : 1 + step_z + width_z,
    ]


def edge_weights(tensors, step_x, step_y, step_z, component, factor):
    layer = tensors[component]
    return 0.5 * factor * (shifted(layer, 0, 0, 0) + shifted(layer, step_x, step_y, step_z))


def operate(padded, tensors):
    centre = shifted(padded, 0, 0, 0)
    accumulated = jnp.zeros_like(centre)
    for step_x, step_y, step_z, component, factor in STENCIL_TAPS:
        weight = edge_weights(tensors, step_x, step_y, step_z, component, factor)
        accumulated = accumulated + weight * (centre - shifted(padded, step_x, step_y, step_z))
    return accumulated


def class_onehot(labels, count):
    return (labels[..., None] == jnp.arange(count, dtype=jnp.int32)).astype(jnp.float32)


def reach_onehot(length, offset):
    position = jnp.arange(length, dtype=jnp.int32)
    relative = (position + offset) // length + 1
    return (relative[:, None] == jnp.arange(3, dtype=jnp.int32)[None, :]).astype(jnp.float32)


def reach_blocks(length, offset, blocks):
    block_span = length // blocks
    position = jnp.arange(length, dtype=jnp.int32)
    owning = (position // block_span)[:, None] == jnp.arange(blocks, dtype=jnp.int32)[None, :]
    relative = ((position % block_span + offset) // block_span + 1)[:, None] == jnp.arange(
        3, dtype=jnp.int32
    )[None, :]
    return (owning[:, :, None] & relative[:, None, :]).astype(jnp.float32)


def centre_mask():
    places = jnp.arange(3, dtype=jnp.int32)
    return (
        (places[:, None, None] == 1) & (places[None, :, None] == 1) & (places[None, None, :] == 1)
    )


def build_tensors(matches, scale, class_tensor):
    return (
        jnp.stack(
            [
                jnp.sum(
                    jnp.where(matches, class_tensor[component][:, None, None, None], 0.0), axis=0
                )
                for component in range(6)
            ]
        )
        * scale[None]
    )


def body(right_side, fiber_class, conductivity_scale, class_tensor, block_ids):
    highest = lax.Precision.HIGHEST
    kinds = jnp.arange(NCLS, dtype=jnp.int32)
    matches = fiber_class[None] == kinds[:, None, None, None]
    local_tensor = build_tensors(matches, conductivity_scale, class_tensor)
    tensors = padded_2(local_tensor, (("gx", 1), ("gy", 2), ("gz", 3)), 1)
    place_x = lax.axis_index("gx")
    place_y = lax.axis_index("gy")
    place_z = lax.axis_index("gz")
    padded_ids = jnp.pad(block_ids, 1, constant_values=-1)
    window = lax.dynamic_slice(padded_ids, (place_x, place_y, place_z * ZBLK), (3, 3, ZBLK + 2))
    own_hot = class_onehot(window[1, 1, 1 : ZBLK + 1], COARSE)
    neighbours = jnp.stack([window[:, :, z_block : z_block + 3] for z_block in range(ZBLK)])
    rim_weight = jnp.zeros((ZBLK, 3, 3, 3), jnp.float32)
    for step_x, step_y, step_z, component, factor in STENCIL_TAPS:
        weight = edge_weights(tensors, step_x, step_y, step_z, component, factor)
        rim_weight = rim_weight + jnp.einsum(
            "xyz,xa,yb,zjc->jabc",
            weight,
            reach_onehot(CX, step_x),
            reach_onehot(CY, step_y),
            reach_blocks(CZ, step_z, ZBLK),
            precision=highest,
        )
    rim_weight = jnp.where(centre_mask()[None], 0.0, rim_weight)
    diagonal_terms = jnp.einsum(
        "jk,j->k", own_hot, jnp.sum(rim_weight, axis=(1, 2, 3)), precision=highest
    )
    coupling = jnp.einsum(
        "jk,jabc,jabcl->kl",
        own_hot,
        rim_weight,
        class_onehot(neighbours, COARSE),
        precision=highest,
    )
    coarse = lax.psum(jnp.diag(diagonal_terms) - coupling, ("gx", "gy", "gz"))
    coarse = 0.5 * (coarse + coarse.T)
    factor_lower = jnp.linalg.cholesky(coarse)

    def restrict(field):
        block_totals = jnp.sum(field.reshape(CX, CY, ZBLK, BZ), axis=(0, 1, 3))
        return jnp.einsum("jk,j->k", own_hot, block_totals, precision=highest)

    def prolong(coarse_values):
        values = jnp.einsum("jk,k->j", own_hot, coarse_values, precision=highest)
        return jnp.broadcast_to(values[None, None, :, None], (CX, CY, ZBLK, BZ)).reshape(CX, CY, CZ)

    def apply_field(field):
        padded = padded_2(field, (("gx", 0), ("gy", 1), ("gz", 2)), 1)
        return operate(padded, tensors)

    def coarse_solve(field):
        projected = lax.psum(restrict(field), ("gx", "gy", "gz"))
        return jax.scipy.linalg.cho_solve((factor_lower, True), projected)

    def deflation_image(coarse_values):
        result = apply_field(prolong(coarse_values))
        return result

    coarse_values = coarse_solve(right_side)
    coarse_part = prolong(coarse_values)
    residual = right_side - deflation_image(coarse_values)
    estimate = jnp.zeros_like(right_side)

    def joint_terms(field):
        product = apply_field(field)
        projected, norm_value, cross_value = lax.psum(
            (restrict(product), jnp.sum(field * field), jnp.sum(field * product)),
            ("gx", "gy", "gz"),
        )
        correction = jax.scipy.linalg.cho_solve((factor_lower, True), projected)
        image_field = product - deflation_image(correction)
        return (image_field, norm_value, cross_value - jnp.sum(projected * correction))

    image_field, norm_now, curvature_now = joint_terms(residual)
    step_size = norm_now / curvature_now
    direction = residual
    along = image_field
    for iteration in range(ITERS):
        estimate = estimate + step_size * direction
        residual = residual - step_size * along
        if iteration + 1 < ITERS:
            image_field, norm_next, curvature_now = joint_terms(residual)
            step_ratio = norm_next / norm_now
            step_size = norm_next / (curvature_now - step_ratio * norm_next / step_size)
            direction = residual + step_ratio * direction
            along = image_field + step_ratio * along
            norm_now = norm_next
    solution = coarse_part + estimate - prolong(coarse_solve(apply_field(estimate)))
    return (solution, residual)


def solution(mesh):
    placed = (P("gx", "gy", "gz"), P("gx", "gy", "gz"), P("gx", "gy", "gz"), P(), P())
    return jax.shard_map(
        body,
        mesh=mesh,
        in_specs=placed,
        out_specs=(P("gx", "gy", "gz"), P("gx", "gy", "gz")),
        check_vma=False,
    )
```

profile of v0, /device:TPU:0, one launch (start us, length us, event | category | flops | bytes accessed | tf_op | source)
XLA Modules:
  0.0 365.0 jit_solution(11324183408643841926)
XLA Ops:
  4.2 4.9 %collective-permute-start = (f32[6,1,16,128]{3,2,1,0:T(8,128)S(1)}, f32[6,1,16,128]{3,2,1,0:T(8,128)S(1)}, u32[]{:S(2)}, u32[]{:S(2)}) collective-permute-start(f32[6,1,16,128]{3,2,1,0:T(8,128)S(1)} %get-tuple-element.39), channel_id=1, source_target_pairs={{0,16},{1,17},{2,18},{3,19},{4,20},{5,21},{6,22},{7,23},{8,24},{9,... | collective-permute-start | bytes 147464 | tf_op jit(solution)/shard_map/ppermute | solution.py:46
  11.4 3.7 %collective-permute-done.1 = f32[6,1,16,128]{3,2,1,0:T(8,128)S(1)} collective-permute-done((f32[6,1,16,128]{3,2,1,0:T(8,128)S(1)}, f32[6,1,16,128]{3,2,1,0:T(8,128)S(1)}, u32[]{:S(2)}, u32[]{:S(2)}) %collective-permute-start.1) | collective-permute-done | bytes 49184 | tf_op jit(solution)/shard_map/ppermute | solution.py:48
  15.1 3.5 collective-permute-start.2
  20.2 4.2 %collective-permute-done.3 = f32[6,10,1,128]{3,2,1,0:T(1,128)S(1)} collective-permute-done((f32[6,10,1,128]{3,2,1,0:T(1,128)S(1)}, f32[6,10,1,128]{3,2,1,0:T(1,128)S(1)}, u32[]{:S(2)}, u32[]{:S(2)}) %collective-permute-start.3) | collective-permute-done | bytes 30752 | tf_op jit(solution)/shard_map/ppermute | solution.py:48
  43.4 40.4 %all-reduce.3 = (f32[64,64]{1,0:T(8,128)S(1)}, f32[64]{0:T(128)S(1)}) all-reduce(f32[64,64]{1,0:T(8,128)S(1)} %convolution_subtract_fusion, f32[64]{0:T(128)S(1)} %convolution_bitcast_fusion.26), channel_id=1, replica_groups=mesh['gx'=2,'gy'=4,'gz'=4] {'gx','gy','gz'}, use_global_device_ids=true, to_apply=%region_7.8 | all-reduce | flops 4160 | bytes 33280 | tf_op jit(solution)/shard_map/psum | solution.py:156
  84.0 5.8 %cholesky.19 = f32[64,64]{1,0:T(8,128)S(1)} custom-call(f32[64,64]{1,0:T(8,128)S(1)} %fusion.262), custom_call_target="Cholesky" | custom-call | tf_op jit(solution)/shard_map/jit(cholesky)/cholesky | solution.py:158
  91.2 4.9 %custom-call.11 = f32[1,64,64]{1,2,0:T(8,128)S(1)} custom-call(f32[1,64,64]{2,1,0:T(8,128)S(1)} %fusion.251), custom_call_target="InvertDiagBlocksLowerTriangular" | custom-call | tf_op jit(solution)/shard_map/jit(_cho_solve)/triangular_solve | solution.py:174
  98.1 4.5 %collective-permute-start.7 = (f32[1,16,128]{2,1,0:T(8,128)S(1)}, f32[1,16,128]{2,1,0:T(8,128)S(1)}, u32[]{:S(2)}, u32[]{:S(2)}) collective-permute-start(f32[1,16,128]{2,1,0:T(8,128)S(1)} %slice.1082), channel_id=1, source_target_pairs={{0,16},{1,17},{2,18},{3,19},{4,20},{5,21},{6,22},{7,23},{8,24},{9,... | collective-permute-start | bytes 24584 | tf_op jit(solution)/shard_map/ppermute | solution.py:46
  105.3 4.5 %collective-permute-start.9 = (f32[10,1,128]{2,1,0:T(1,128)S(1)}, f32[10,1,128]{2,1,0:T(1,128)S(1)}, u32[]{:S(2)}, u32[]{:S(2)}) collective-permute-start(f32[10,1,128]{2,1,0:T(1,128)S(1)} %get-tuple-element.105), channel_id=1, source_target_pairs={{0,4},{4,8},{8,12},{1,5},{5,9},{9,13},{2,6},{6,10},{10,14},{3,7},{... | collective-permute-start | bytes 15368 | tf_op jit(solution)/shard_map/ppermute | solution.py:46
  118.3 4.5 %collective-permute-start.13 = (f32[1,16,128]{2,1,0:T(8,128)S(1)}, f32[1,16,128]{2,1,0:T(8,128)S(1)}, u32[]{:S(2)}, u32[]{:S(2)}) collective-permute-start(f32[1,16,128]{2,1,0:T(8,128)S(1)} %get-tuple-element.111), channel_id=1, source_target_pairs={{0,16},{1,17},{2,18},{3,19},{4,20},{5,21},{6,22},{7,23},{8,24},{9,... | collective-permute-start | bytes 24584 | tf_op jit(solution)/shard_map/ppermute | solution.py:46
  125.5 4.8 %collective-permute-start.15 = (f32[10,1,128]{2,1,0:T(1,128)S(1)}, f32[10,1,128]{2,1,0:T(1,128)S(1)}, u32[]{:S(2)}, u32[]{:S(2)}) collective-permute-start(f32[10,1,128]{2,1,0:T(1,128)S(1)} %get-tuple-element.101), channel_id=1, source_target_pairs={{0,4},{4,8},{8,12},{1,5},{5,9},{9,13},{2,6},{6,10},{10,14},{3,7},{... | collective-permute-start | bytes 15368 | tf_op jit(solution)/shard_map/ppermute | solution.py:46
  133.1 3.3 collective-permute-start.17
  138.8 48.9 %all-reduce.2 = (f32[64]{0:T(128)S(1)}, f32[]{:T(128)}, f32[]{:T(128)}) all-reduce(f32[64]{0:T(128)S(1)} %convolution_bitcast_fusion.24, f32[]{:T(128)} %get-tuple-element.10, f32[]{:T(128)} %get-tuple-element.8), channel_id=1, replica_groups=mesh['gx'=2,'gy'=4,'gz'=4] {'gx','gy','gz'}, use_global_device_ids=true, to_apply=%region_19.21 | all-reduce | flops 66 | bytes 528 | tf_op jit(solution)/shard_map/psum | solution.py:187
  190.3 4.5 %collective-permute-start.19 = (f32[1,16,128]{2,1,0:T(8,128)S(1)}, f32[1,16,128]{2,1,0:T(8,128)S(1)}, u32[]{:S(2)}, u32[]{:S(2)}) collective-permute-start(f32[1,16,128]{2,1,0:T(8,128)S(1)} %slice.1129), channel_id=1, source_target_pairs={{0,16},{1,17},{2,18},{3,19},{4,20},{5,21},{6,22},{7,23},{8,24},{9,... | collective-permute-start | bytes 24584 | tf_op jit(solution)/shard_map/ppermute | solution.py:46
  197.5 4.5 %collective-permute-start.21 = (f32[10,1,128]{2,1,0:T(1,128)S(1)}, f32[10,1,128]{2,1,0:T(1,128)S(1)}, u32[]{:S(2)}, u32[]{:S(2)}) collective-permute-start(f32[10,1,128]{2,1,0:T(1,128)S(1)} %get-tuple-element.97), channel_id=1, source_target_pairs={{0,4},{4,8},{8,12},{1,5},{5,9},{9,13},{2,6},{6,10},{10,14},{3,7},{... | collective-permute-start | bytes 15368 | tf_op jit(solution)/shard_map/ppermute | solution.py:46
  211.2 4.5 %collective-permute-start.25 = (f32[1,16,128]{2,1,0:T(8,128)S(1)}, f32[1,16,128]{2,1,0:T(8,128)S(1)}, u32[]{:S(2)}, u32[]{:S(2)}) collective-permute-start(f32[1,16,128]{2,1,0:T(8,128)S(1)} %get-tuple-element.109), channel_id=1, source_target_pairs={{0,16},{1,17},{2,18},{3,19},{4,20},{5,21},{6,22},{7,23},{8,24},{9,... | collective-permute-start | bytes 24584 | tf_op jit(solution)/shard_map/ppermute | solution.py:46
  218.4 4.5 %collective-permute-start.27 = (f32[10,1,128]{2,1,0:T(1,128)S(1)}, f32[10,1,128]{2,1,0:T(1,128)S(1)}, u32[]{:S(2)}, u32[]{:S(2)}) collective-permute-start(f32[10,1,128]{2,1,0:T(1,128)S(1)} %get-tuple-element.93), channel_id=1, source_target_pairs={{0,4},{4,8},{8,12},{1,5},{5,9},{9,13},{2,6},{6,10},{10,14},{3,7},{... | collective-permute-start | bytes 15368 | tf_op jit(solution)/shard_map/ppermute | solution.py:46
  231.3 48.6 %all-reduce.1 = (f32[]{:T(128)}, f32[]{:T(128)}, f32[64]{0:T(128)S(1)}) all-reduce(f32[]{:T(128)} %get-tuple-element.7, f32[]{:T(128)} %get-tuple-element.6, f32[64]{0:T(128)S(1)} %convolution_bitcast_fusion.22), channel_id=1, replica_groups=mesh['gx'=2,'gy'=4,'gz'=4] {'gx','gy','gz'}, use_global_device_ids=true, to_apply=%region_22.24 | all-reduce | flops 66 | bytes 528 | tf_op jit(solution)/shard_map/psum | solution.py:187
  282.6 4.5 %collective-permute-start.37 = (f32[1,16,128]{2,1,0:T(8,128)S(1)}, f32[1,16,128]{2,1,0:T(8,128)S(1)}, u32[]{:S(2)}, u32[]{:S(2)}) collective-permute-start(f32[1,16,128]{2,1,0:T(8,128)S(1)} %slice.1200), channel_id=1, source_target_pairs={{0,16},{1,17},{2,18},{3,19},{4,20},{5,21},{6,22},{7,23},{8,24},{9,... | collective-permute-start | bytes 24584 | tf_op jit(solution)/shard_map/ppermute | solution.py:46
  293.0 4.5 %collective-permute-start.31 = (f32[1,16,128]{2,1,0:T(8,128)S(1)}, f32[1,16,128]{2,1,0:T(8,128)S(1)}, u32[]{:S(2)}, u32[]{:S(2)}) collective-permute-start(f32[1,16,128]{2,1,0:T(8,128)S(1)} %get-tuple-element.107), channel_id=1, source_target_pairs={{0,16},{1,17},{2,18},{3,19},{4,20},{5,21},{6,22},{7,23},{8,24},{9,... | collective-permute-start | bytes 24584 | tf_op jit(solution)/shard_map/ppermute | solution.py:46
  298.9 4.5 %collective-permute-start.39 = (f32[10,1,128]{2,1,0:T(1,128)S(1)}, f32[10,1,128]{2,1,0:T(1,128)S(1)}, u32[]{:S(2)}, u32[]{:S(2)}) collective-permute-start(f32[10,1,128]{2,1,0:T(1,128)S(1)} %get-tuple-element.85), channel_id=1, source_target_pairs={{0,4},{4,8},{8,12},{1,5},{5,9},{9,13},{2,6},{6,10},{10,14},{3,7},{... | collective-permute-start | bytes 15368 | tf_op jit(solution)/shard_map/ppermute | solution.py:46
  304.8 4.5 %collective-permute-start.33 = (f32[10,1,128]{2,1,0:T(1,128)S(1)}, f32[10,1,128]{2,1,0:T(1,128)S(1)}, u32[]{:S(2)}, u32[]{:S(2)}) collective-permute-start(f32[10,1,128]{2,1,0:T(1,128)S(1)} %get-tuple-element.89), channel_id=1, source_target_pairs={{0,4},{4,8},{8,12},{1,5},{5,9},{9,13},{2,6},{6,10},{10,14},{3,7},{... | collective-permute-start | bytes 15368 | tf_op jit(solution)/shard_map/ppermute | solution.py:46
  315.3 4.7 %collective-permute-start.35 = (f32[10,18,1]{2,1,0:T(8,128)S(1)}, f32[10,18,1]{2,1,0:T(8,128)S(1)}, u32[]{:S(2)}, u32[]{:S(2)}) collective-permute-start(f32[10,18,1]{2,1,0:T(8,128)S(1)} %get-tuple-element.61), channel_id=1, source_target_pairs={{0,1},{1,2},{2,3},{4,5},{5,6},{6,7},{8,9},{9,10},{10,11},{12,13},{... | collective-permute-start | bytes 2168 | tf_op jit(solution)/shard_map/ppermute | solution.py:46
  321.7 40.9 %psum.71 = f32[64]{0:T(128)S(1)} all-reduce(f32[64]{0:T(128)S(1)} %convolution_bitcast_fusion.21), channel_id=1, replica_groups=mesh['gx'=2,'gy'=4,'gz'=4] {'gx','gy','gz'}, use_global_device_ids=true, to_apply=%region_31.33 | all-reduce | flops 64 | bytes 512 | tf_op jit(solution)/shard_map/psum | solution.py:173
  (256 shorter events, 88.0 us)
Async XLA Ops:
  4.2 7.1 %collective-permute-start = (f32[6,1,16,128]{3,2,1,0:T(8,128)S(1)}, f32[6,1,16,128]{3,2,1,0:T(8,128)S(1)}, u32[]{:S(2)}, u32[]{:S(2)}) collective-permute-start(f32[6,1,16,128]{3,2,1,0:T(8,128)S(1)} %get-tuple-element.39), channel_id=1, source_target_pairs={{0,16},{1,17},{2,18},{3,19},{4,20},{5,21},{6,22},{7,23},{8,24},{9,... | collective-permute-start | bytes 147464 | tf_op jit(solution)/shard_map/ppermute | solution.py:46
  9.1 6.0 %collective-permute-start.1 = (f32[6,1,16,128]{3,2,1,0:T(8,128)S(1)}, f32[6,1,16,128]{3,2,1,0:T(8,128)S(1)}, u32[]{:S(2)}, u32[]{:S(2)}) collective-permute-start(f32[6,1,16,128]{3,2,1,0:T(8,128)S(1)} %get-tuple-element.40), channel_id=1, source_target_pairs={{16,0},{17,1},{18,2},{19,3},{20,4},{21,5},{22,6},{23,7},{24,8},{25... | collective-permute-start | bytes 147464 | tf_op jit(solution)/shard_map/ppermute | solution.py:48
  96.8 5.9 %collective-permute-start.6 = (f32[1,16,128]{2,1,0:T(8,128)S(1)}, f32[1,16,128]{2,1,0:T(8,128)S(1)}, u32[]{:S(2)}, u32[]{:S(2)}) collective-permute-start(f32[1,16,128]{2,1,0:T(8,128)S(1)} %slice.1082), channel_id=1, source_target_pairs={{16,0},{17,1},{18,2},{19,3},{20,4},{21,5},{22,6},{23,7},{24,8},{25... | collective-permute-start | bytes 24584 | tf_op jit(solution)/shard_map/ppermute | solution.py:48
  98.1 5.9 %collective-permute-start.7 = (f32[1,16,128]{2,1,0:T(8,128)S(1)}, f32[1,16,128]{2,1,0:T(8,128)S(1)}, u32[]{:S(2)}, u32[]{:S(2)}) collective-permute-start(f32[1,16,128]{2,1,0:T(8,128)S(1)} %slice.1082), channel_id=1, source_target_pairs={{0,16},{1,17},{2,18},{3,19},{4,20},{5,21},{6,22},{7,23},{8,24},{9,... | collective-permute-start | bytes 24584 | tf_op jit(solution)/shard_map/ppermute | solution.py:46
  105.3 5.9 %collective-permute-start.9 = (f32[10,1,128]{2,1,0:T(1,128)S(1)}, f32[10,1,128]{2,1,0:T(1,128)S(1)}, u32[]{:S(2)}, u32[]{:S(2)}) collective-permute-start(f32[10,1,128]{2,1,0:T(1,128)S(1)} %get-tuple-element.105), channel_id=1, source_target_pairs={{0,4},{4,8},{8,12},{1,5},{5,9},{9,13},{2,6},{6,10},{10,14},{3,7},{... | collective-permute-start | bytes 15368 | tf_op jit(solution)/shard_map/ppermute | solution.py:46
  118.3 5.9 %collective-permute-start.13 = (f32[1,16,128]{2,1,0:T(8,128)S(1)}, f32[1,16,128]{2,1,0:T(8,128)S(1)}, u32[]{:S(2)}, u32[]{:S(2)}) collective-permute-start(f32[1,16,128]{2,1,0:T(8,128)S(1)} %get-tuple-element.111), channel_id=1, source_target_pairs={{0,16},{1,17},{2,18},{3,19},{4,20},{5,21},{6,22},{7,23},{8,24},{9,... | collective-permute-start | bytes 24584 | tf_op jit(solution)/shard_map/ppermute | solution.py:46
  124.2 6.1 %collective-permute-start.14 = (f32[10,1,128]{2,1,0:T(1,128)S(1)}, f32[10,1,128]{2,1,0:T(1,128)S(1)}, u32[]{:S(2)}, u32[]{:S(2)}) collective-permute-start(f32[10,1,128]{2,1,0:T(1,128)S(1)} %get-tuple-element.102), channel_id=1, source_target_pairs={{4,0},{8,4},{12,8},{5,1},{9,5},{13,9},{6,2},{10,6},{14,10},{7,3},{... | collective-permute-start | bytes 15368 | tf_op jit(solution)/shard_map/ppermute | solution.py:48
  125.5 6.1 %collective-permute-start.15 = (f32[10,1,128]{2,1,0:T(1,128)S(1)}, f32[10,1,128]{2,1,0:T(1,128)S(1)}, u32[]{:S(2)}, u32[]{:S(2)}) collective-permute-start(f32[10,1,128]{2,1,0:T(1,128)S(1)} %get-tuple-element.101), channel_id=1, source_target_pairs={{0,4},{4,8},{8,12},{1,5},{5,9},{9,13},{2,6},{6,10},{10,14},{3,7},{... | collective-permute-start | bytes 15368 | tf_op jit(solution)/shard_map/ppermute | solution.py:46
  190.3 5.9 %collective-permute-start.19 = (f32[1,16,128]{2,1,0:T(8,128)S(1)}, f32[1,16,128]{2,1,0:T(8,128)S(1)}, u32[]{:S(2)}, u32[]{:S(2)}) collective-permute-start(f32[1,16,128]{2,1,0:T(8,128)S(1)} %slice.1129), channel_id=1, source_target_pairs={{0,16},{1,17},{2,18},{3,19},{4,20},{5,21},{6,22},{7,23},{8,24},{9,... | collective-permute-start | bytes 24584 | tf_op jit(solution)/shard_map/ppermute | solution.py:46
  196.2 7.8 %collective-permute-start.20 = (f32[10,1,128]{2,1,0:T(1,128)S(1)}, f32[10,1,128]{2,1,0:T(1,128)S(1)}, u32[]{:S(2)}, u32[]{:S(2)}) collective-permute-start(f32[10,1,128]{2,1,0:T(1,128)S(1)} %get-tuple-element.98), channel_id=1, source_target_pairs={{4,0},{8,4},{12,8},{5,1},{9,5},{13,9},{6,2},{10,6},{14,10},{7,3},{... | collective-permute-start | bytes 15368 | tf_op jit(solution)/shard_map/ppermute | solution.py:48
  197.5 6.5 %collective-permute-start.21 = (f32[10,1,128]{2,1,0:T(1,128)S(1)}, f32[10,1,128]{2,1,0:T(1,128)S(1)}, u32[]{:S(2)}, u32[]{:S(2)}) collective-permute-start(f32[10,1,128]{2,1,0:T(1,128)S(1)} %get-tuple-element.97), channel_id=1, source_target_pairs={{0,4},{4,8},{8,12},{1,5},{5,9},{9,13},{2,6},{6,10},{10,14},{3,7},{... | collective-permute-start | bytes 15368 | tf_op jit(solution)/shard_map/ppermute | solution.py:46
  211.2 5.9 %collective-permute-start.25 = (f32[1,16,128]{2,1,0:T(8,128)S(1)}, f32[1,16,128]{2,1,0:T(8,128)S(1)}, u32[]{:S(2)}, u32[]{:S(2)}) collective-permute-start(f32[1,16,128]{2,1,0:T(8,128)S(1)} %get-tuple-element.109), channel_id=1, source_target_pairs={{0,16},{1,17},{2,18},{3,19},{4,20},{5,21},{6,22},{7,23},{8,24},{9,... | collective-permute-start | bytes 24584 | tf_op jit(solution)/shard_map/ppermute | solution.py:46
  218.4 5.9 %collective-permute-start.27 = (f32[10,1,128]{2,1,0:T(1,128)S(1)}, f32[10,1,128]{2,1,0:T(1,128)S(1)}, u32[]{:S(2)}, u32[]{:S(2)}) collective-permute-start(f32[10,1,128]{2,1,0:T(1,128)S(1)} %get-tuple-element.93), channel_id=1, source_target_pairs={{0,4},{4,8},{8,12},{1,5},{5,9},{9,13},{2,6},{6,10},{10,14},{3,7},{... | collective-permute-start | bytes 15368 | tf_op jit(solution)/shard_map/ppermute | solution.py:46
  281.3 16.3 %collective-permute-start.36 = (f32[1,16,128]{2,1,0:T(8,128)S(1)}, f32[1,16,128]{2,1,0:T(8,128)S(1)}, u32[]{:S(2)}, u32[]{:S(2)}) collective-permute-start(f32[1,16,128]{2,1,0:T(8,128)S(1)} %slice.1200), channel_id=1, source_target_pairs={{16,0},{17,1},{18,2},{19,3},{20,4},{21,5},{22,6},{23,7},{24,8},{25... | collective-permute-start | bytes 24584 | tf_op jit(solution)/shard_map/ppermute | solution.py:48
  282.6 15.0 %collective-permute-start.37 = (f32[1,16,128]{2,1,0:T(8,128)S(1)}, f32[1,16,128]{2,1,0:T(8,128)S(1)}, u32[]{:S(2)}, u32[]{:S(2)}) collective-permute-start(f32[1,16,128]{2,1,0:T(8,128)S(1)} %slice.1200), channel_id=1, source_target_pairs={{0,16},{1,17},{2,18},{3,19},{4,20},{5,21},{6,22},{7,23},{8,24},{9,... | collective-permute-start | bytes 24584 | tf_op jit(solution)/shard_map/ppermute | solution.py:46
  291.7 11.8 %collective-permute-start.30 = (f32[1,16,128]{2,1,0:T(8,128)S(1)}, f32[1,16,128]{2,1,0:T(8,128)S(1)}, u32[]{:S(2)}, u32[]{:S(2)}) collective-permute-start(f32[1,16,128]{2,1,0:T(8,128)S(1)} %get-tuple-element.108), channel_id=1, source_target_pairs={{16,0},{17,1},{18,2},{19,3},{20,4},{21,5},{22,6},{23,7},{24,8},{25... | collective-permute-start | bytes 24584 | tf_op jit(solution)/shard_map/ppermute | solution.py:48
  293.0 10.5 %collective-permute-start.31 = (f32[1,16,128]{2,1,0:T(8,128)S(1)}, f32[1,16,128]{2,1,0:T(8,128)S(1)}, u32[]{:S(2)}, u32[]{:S(2)}) collective-permute-start(f32[1,16,128]{2,1,0:T(8,128)S(1)} %get-tuple-element.107), channel_id=1, source_target_pairs={{0,16},{1,17},{2,18},{3,19},{4,20},{5,21},{6,22},{7,23},{8,24},{9,... | collective-permute-start | bytes 24584 | tf_op jit(solution)/shard_map/ppermute | solution.py:46
  297.6 11.8 %collective-permute-start.38 = (f32[10,1,128]{2,1,0:T(1,128)S(1)}, f32[10,1,128]{2,1,0:T(1,128)S(1)}, u32[]{:S(2)}, u32[]{:S(2)}) collective-permute-start(f32[10,1,128]{2,1,0:T(1,128)S(1)} %get-tuple-element.86), channel_id=1, source_target_pairs={{4,0},{8,4},{12,8},{5,1},{9,5},{13,9},{6,2},{10,6},{14,10},{7,3},{... | collective-permute-start | bytes 15368 | tf_op jit(solution)/shard_map/ppermute | solution.py:48
  298.9 10.5 %collective-permute-start.39 = (f32[10,1,128]{2,1,0:T(1,128)S(1)}, f32[10,1,128]{2,1,0:T(1,128)S(1)}, u32[]{:S(2)}, u32[]{:S(2)}) collective-permute-start(f32[10,1,128]{2,1,0:T(1,128)S(1)} %get-tuple-element.85), channel_id=1, source_target_pairs={{0,4},{4,8},{8,12},{1,5},{5,9},{9,13},{2,6},{6,10},{10,14},{3,7},{... | collective-permute-start | bytes 15368 | tf_op jit(solution)/shard_map/ppermute | solution.py:46
  303.5 10.3 %collective-permute-start.32 = (f32[10,1,128]{2,1,0:T(1,128)S(1)}, f32[10,1,128]{2,1,0:T(1,128)S(1)}, u32[]{:S(2)}, u32[]{:S(2)}) collective-permute-start(f32[10,1,128]{2,1,0:T(1,128)S(1)} %get-tuple-element.90), channel_id=1, source_target_pairs={{4,0},{8,4},{12,8},{5,1},{9,5},{13,9},{6,2},{10,6},{14,10},{7,3},{... | collective-permute-start | bytes 15368 | tf_op jit(solution)/shard_map/ppermute | solution.py:48
  304.8 9.1 %collective-permute-start.33 = (f32[10,1,128]{2,1,0:T(1,128)S(1)}, f32[10,1,128]{2,1,0:T(1,128)S(1)}, u32[]{:S(2)}, u32[]{:S(2)}) collective-permute-start(f32[10,1,128]{2,1,0:T(1,128)S(1)} %get-tuple-element.89), channel_id=1, source_target_pairs={{0,4},{4,8},{8,12},{1,5},{5,9},{9,13},{2,6},{6,10},{10,14},{3,7},{... | collective-permute-start | bytes 15368 | tf_op jit(solution)/shard_map/ppermute | solution.py:46
  309.5 54.4 %collective-permute-start.40 = (f32[10,18,1]{2,1,0:T(8,128)S(1)}, f32[10,18,1]{2,1,0:T(8,128)S(1)}, u32[]{:S(2)}, u32[]{:S(2)}) collective-permute-start(f32[10,18,1]{2,1,0:T(8,128)S(1)} %get-tuple-element.60), channel_id=1, source_target_pairs={{1,0},{2,1},{3,2},{5,4},{6,5},{7,6},{9,8},{10,9},{11,10},{13,12},{... | collective-permute-start | bytes 2168 | tf_op jit(solution)/shard_map/ppermute | solution.py:48
  310.8 53.1 %collective-permute-start.41 = (f32[10,18,1]{2,1,0:T(8,128)S(1)}, f32[10,18,1]{2,1,0:T(8,128)S(1)}, u32[]{:S(2)}, u32[]{:S(2)}) collective-permute-start(f32[10,18,1]{2,1,0:T(8,128)S(1)} %get-tuple-element.59), channel_id=1, source_target_pairs={{0,1},{1,2},{2,3},{4,5},{5,6},{6,7},{8,9},{9,10},{10,11},{12,13},{... | collective-permute-start | bytes 2168 | tf_op jit(solution)/shard_map/ppermute | solution.py:46
  314.0 6.0 %collective-permute-start.34 = (f32[10,18,1]{2,1,0:T(8,128)S(1)}, f32[10,18,1]{2,1,0:T(8,128)S(1)}, u32[]{:S(2)}, u32[]{:S(2)}) collective-permute-start(f32[10,18,1]{2,1,0:T(8,128)S(1)} %get-tuple-element.62), channel_id=1, source_target_pairs={{1,0},{2,1},{3,2},{5,4},{6,5},{7,6},{9,8},{10,9},{11,10},{13,12},{... | collective-permute-start | bytes 2168 | tf_op jit(solution)/shard_map/ppermute | solution.py:48
  (20 other events, 108.5 us)
where the time goes:
time: 367 us; the launch traced here: 365 us
  blocking collectives  179 us (49%)
  starting transfers between devices  112 us (31%)
  waiting for transfers between devices  25.1 us (7%)
  other arithmetic  22.3 us (6%)
  matrix products  13.4 us (4%)
  between operations  8.31 us (2%)
  local copies, waits for them, and re-layouts  5.09 us (1%)
    psum x2, blocking collectives, joint_terms(): lax.psum((restrict(product), jnp.sum(field * field), jnp.sum(field * prod...  97.5 us
    ppermute x21, starting transfers between devices, padded_2(): lax.ppermute(tail, axis, [(i, (i + 1) % count) for i in range(ends)])  84.8 us
    psum x1, blocking collectives, coarse_solve(): projected = lax.psum(restrict(field), ('gx', 'gy', 'gz'))  40.9 us
    psum x1, blocking collectives, body(): coarse = lax.psum(jnp.diag(diagonal_terms) - coupling, ('gx', 'gy', 'gz'))  40.4 us
    ppermute x21, starting transfers between devices, padded_2(): lax.ppermute(head, axis, [((i + 1) % count, i) for i in range(ends)])  27.1 us
    ppermute x21, waiting for transfers between devices, padded_2(): lax.ppermute(tail, axis, [(i, (i + 1) % count) for i in range(ends)])  14.1 us
    ppermute x21, waiting for transfers between devices, padded_2(): lax.ppermute(head, axis, [((i + 1) % count, i) for i in range(ends)])  11 us
    dot_general x54, matrix products, body(): jnp.einsum('xyz,xa,yb,zjc->jabc', weight, reach_onehot(CX, step_x), reach...  8.59 us
  transfers between devices with their start and end apart: 42, of which 16 were waited for; matrix products, arithmetic and copies ran while one was open for 1% of the time, Pallas kernels for 0%

commit v1 on v0

v1 whole, which is shorter than its diff:
```python
import functools

import jax
import jax.numpy as jnp
from jax import lax
from jax.experimental import pallas as pl
from jax.experimental.pallas import tpu as pltpu
from jax.sharding import PartitionSpec as P

COARSE = 64
LANES = 128
HIGHEST = lax.Precision.HIGHEST
MESH = pl.DeviceIdType.MESH
F32 = jnp.float32

XX, XZ, XY, YY, YZ, ZZ = range(6)
TABLE_ROW = {XX: 0, YY: 1, ZZ: 2, XY: 3, XZ: 4, YZ: 5}
ZSLOT = {XZ: 0, YZ: 1, ZZ: 2}

TAPS = (
    (1, 0, 0, XX, 0.5),
    (-1, 0, 0, XX, 0.5),
    (0, 1, 0, YY, 0.5),
    (0, -1, 0, YY, 0.5),
    (0, 0, 1, ZZ, 0.5),
    (0, 0, -1, ZZ, 0.5),
    (1, 1, 0, XY, 0.25),
    (-1, -1, 0, XY, 0.25),
    (1, -1, 0, XY, -0.25),
    (-1, 1, 0, XY, -0.25),
    (1, 0, 1, XZ, 0.25),
    (-1, 0, -1, XZ, 0.25),
    (1, 0, -1, XZ, -0.25),
    (-1, 0, 1, XZ, -0.25),
    (0, 1, 1, YZ, 0.25),
    (0, -1, -1, YZ, 0.25),
    (0, 1, -1, YZ, -0.25),
    (0, -1, 1, YZ, -0.25),
)
OFFSETS = tuple(tap[:3] for tap in TAPS)
SLOT = {offset: i for i, offset in enumerate(OFFSETS)}
ZOFFSETS = tuple(o for o in OFFSETS if o[2])
ZINDEX = {offset: i for i, offset in enumerate(ZOFFSETS)}
XYOFFSETS = tuple(o for o in OFFSETS if o[0] and o[1])
XYINDEX = {offset: i for i, offset in enumerate(XYOFFSETS)}
TOP = 8


def neg(offset):
    return tuple(-s for s in offset)


def iota(shape, dim):
    return lax.broadcasted_iota(jnp.int32, shape, dim)


def kernel(
    dims,
    ids_ref,
    table_ref,
    right_ref,
    class_ref,
    scale_ref,
    sol_ref,
    res_ref,
    tens,
    tens_p,
    tens_m,
    weight,
    field,
    field_p,
    field_m,
    prod,
    image,
    rim,
    inverse,
    t_ypack,
    t_yr,
    t_xyr,
    t_zpack,
    t_zr,
    f_ypack,
    f_yr,
    f_xyr,
    f_zpack,
    f_zr,
    msg1,
    gat1,
    den1,
    msg2,
    gat2,
    den2,
    halo_send,
    halo_recv,
    gat_send,
    gat_recv,
):
    nx, ny, nz, bx, by, zblk, nbx, nby, nbz = dims
    bz = LANES
    span = bz // zblk
    count = nx * ny * nz
    px, py, pz = lax.axis_index("gx"), lax.axis_index("gy"), lax.axis_index("gz")
    me = (px * ny + py) * nz + pz
    rows = slice(TOP, TOP + by)
    own = slice(1, 1 + bx)

    tens[0:3, 0, rows, :] = jnp.zeros((3, by, bz), F32)
    tens[0:3, bx + 1, rows, :] = jnp.zeros((3, by, bz), F32)
    for e in range(2):
        field[e, 0, rows, :] = jnp.zeros((by, bz), F32)
        field[e, bx + 1, rows, :] = jnp.zeros((by, bz), F32)
    for buffer in (t_yr, t_xyr, t_zr, f_yr, f_xyr, f_zr):
        buffer[...] = jnp.zeros(buffer.shape, F32)

    def other(d):
        t = lax.rem(me + d, count)
        return (lax.div(t, ny * nz), lax.rem(lax.div(t, nz), ny), lax.rem(t, nz))

    barrier = pltpu.get_barrier_semaphore()

    @pl.loop(1, count)
    def _(d):
        pl.semaphore_signal(barrier, inc=1, device_id=other(d), device_id_type=MESH)

    lane1 = iota((1, bz), 1)
    place = lane1 % span
    block = lane1 // span
    first, last = place == 0, place == span - 1

    def read_id(x, y, z):
        inside = (x >= 0) & (x < nbx) & (y >= 0) & (y < nby) & (z >= 0) & (z < nbz)
        value = ids_ref[
            jnp.clip(x, 0, nbx - 1), jnp.clip(y, 0, nby - 1), jnp.clip(z, 0, nbz - 1)
        ]
        return jnp.where(inside, value, COARSE)

    window = {}
    for dx in range(3):
        for dy in range(3):
            for dz in range(zblk + 2):
                window[dx, dy, dz] = read_id(px + dx - 1, py + dy - 1, pz * zblk + dz - 1)
    around = []
    row48 = iota((48, LANES), 0)
    lane48 = iota((48, LANES), 1)
    for j in range(zblk):
        ids = jnp.full((48, LANES), -1, jnp.int32)
        for dz in range(3):
            for dx in range(3):
                for dy in range(3):
                    ids = jnp.where(
                        row48 == dz * 16 + dx * 3 + dy, window[dx, dy, j + dz], ids
                    )
        around.append((ids == lane48).astype(F32))
    own_id = [window[1, 1, j + 1] for j in range(zblk)]

    for x in range(bx):
        kind = class_ref[x]
        parts = [jnp.full((by, bz), table_ref[c, 0], F32) for c in range(6)]
        for k in range(1, table_ref.shape[1]):
            match = kind == k
            parts = [jnp.where(match, table_ref[c, k], parts[c]) for c in range(6)]
        for slot in range(6):
            tens[slot, 1 + x, rows, :] = parts[TABLE_ROW[slot]] * scale_ref[x]

    def own_tensor(slot):
        return tens[slot, own, rows, :]

    def halves(row):
        return [
            jnp.sum(jnp.where(block == j, row, 0.0), axis=1, keepdims=True) for j in range(zblk)
        ]

    def plane_sum(slot, x):
        return jnp.sum(tens[slot, 1 + x, rows, :], axis=0, keepdims=True)

    def line_sum(slot, y):
        total = tens[slot, 1, TOP + y : TOP + y + 1, :]
        for x in range(1, bx):
            total = total + tens[slot, 1 + x, TOP + y : TOP + y + 1, :]
        return total

    def corner(x, y):
        return tens[XY, 1 + x, TOP + y : TOP + y + 1, :]

    hi_x, hi_y = bx - 1, by - 1
    c00, c01, c10, c11 = corner(0, 0), corner(0, hi_y), corner(hi_x, 0), corner(hi_x, hi_y)
    xz_lo, xz_hi = plane_sum(XZ, 0), plane_sum(XZ, hi_x)
    yz_lo, yz_hi = line_sum(YZ, 0), line_sum(YZ, hi_y)
    zz_all = jnp.sum(jnp.sum(own_tensor(ZZ), axis=0), axis=0, keepdims=True)
    flat = {
        (1, 0): 0.5 * plane_sum(XX, hi_x) + 0.25 * (c10 - c11),
        (-1, 0): 0.5 * plane_sum(XX, 0) + 0.25 * (c01 - c00),
        (0, 1): 0.5 * line_sum(YY, hi_y) + 0.25 * (c01 - c11),
        (0, -1): 0.5 * line_sum(YY, 0) + 0.25 * (c10 - c00),
        (1, 1): 0.25 * c11,
        (-1, -1): 0.25 * c00,
        (1, -1): -0.25 * c10,
        (-1, 1): -0.25 * c01,
    }
    tilted = {
        (1, 0): 0.25 * xz_hi,
        (-1, 0): -0.25 * xz_lo,
        (0, 1): 0.25 * yz_hi,
        (0, -1): -0.25 * yz_lo,
    }
    slant = 0.25 * (xz_lo - xz_hi + yz_lo - yz_hi)
    rim[...] = jnp.zeros(rim.shape, F32)
    for key, row in flat.items():
        at = (key[0] + 1) * 3 + key[1] + 1
        if key in tilted:
            up = jnp.where(last, tilted[key], 0.0)
            down = jnp.where(first, -tilted[key], 0.0)
            rim[at : at + 1, :] = down
            rim[32 + at : 33 + at, :] = up
            row = row - up - down
        rim[16 + at : 17 + at, :] = row
    rim[4:5, :] = jnp.where(first, 0.5 * zz_all - slant, 0.0)
    rim[36:37, :] = jnp.where(last, 0.5 * zz_all + slant, 0.0)

    sums = jnp.sum(jnp.sum(right_ref[...], axis=0), axis=0, keepdims=True)
    totals = halves(sums)
    block48 = lane48 // span
    for j in range(zblk):
        leaving = jnp.sum(jnp.where(block48 == j, rim[...], 0.0), axis=1, keepdims=True)
        row = jnp.sum(leaving * around[j], axis=0, keepdims=True)
        row = jnp.where(lane1 == COARSE + 1, totals[j], row)
        row = jnp.where(lane1 == COARSE + 2, own_id[j].astype(F32), row)
        msg1[j : j + 1, :] = row
        gat1[me, j : j + 1, :] = row

    lane8, row8 = iota((8, LANES), 1), iota((8, LANES), 0)

    def pick(i):
        return (
            ((row8 == i) & (lane8 == 0)) | ((row8 == i + 3) & (lane8 == bz - 1))
        ).astype(F32)

    def faces(cells, i):
        return lax.dot_general(
            pick(i),
            cells.reshape(bx * by, bz),
            (((1,), (1,)), ((), ())),
            precision=HIGHEST,
            preferred_element_type=F32,
        )

    t_zpack[...] = (
        faces(own_tensor(XZ), 0) + faces(own_tensor(YZ), 1) + faces(own_tensor(ZZ), 2)
    )
    for side, y in ((0, 0), (1, hi_y)):
        for i, slot in enumerate((XY, YY, YZ)):
            for x in range(bx):
                t_ypack[side, i, x : x + 1, :] = tens[slot, 1 + x, TOP + y : TOP + y + 1, :]

    pl.semaphore_wait(barrier, count - 1)

    def spread(msg, gat, g):
        @pl.loop(1, count)
        def _(d):
            pltpu.make_async_remote_copy(
                src_ref=msg,
                dst_ref=gat.at[me],
                send_sem=gat_send.at[g],
                recv_sem=gat_recv.at[g],
                device_id=other(d),
                device_id_type=MESH,
            ).start()

    def gathered(gat, g):
        every = pltpu.make_async_remote_copy(
            src_ref=gat.at[pl.ds(0, count - 1)],
            dst_ref=gat.at[pl.ds(0, count - 1)],
            send_sem=gat_send.at[g],
            recv_sem=gat_recv.at[g],
            device_id=other(1),
            device_id_type=MESH,
        )
        every.wait_send()
        every.wait_recv()

    def exchange(e, ends):
        def copies():
            for offset in OFFSETS:
                dx, dy, dz = offset
                tx, ty, tz = px + dx, py + dy, pz + dz
                inside = None
                for step, at, size in ((dx, tx, nx), (dy, ty, ny), (dz, tz, nz)):
                    if step:
                        ok = (at < size) if step > 0 else (at >= 0)
                        inside = ok if inside is None else inside & ok
                source, target = ends(offset)
                yield inside, pltpu.make_async_remote_copy(
                    src_ref=source,
                    dst_ref=target,
                    send_sem=halo_send.at[e, SLOT[offset]],
                    recv_sem=halo_recv.at[e, SLOT[neg(offset)]],
                    device_id=(tx, ty, tz),
                    device_id_type=MESH,
                )

        def landings():
            for offset in OFFSETS:
                dx, dy, dz = offset
                tx, ty, tz = px + dx, py + dy, pz + dz
                inside = None
                for step, at, size in ((dx, tx, nx), (dy, ty, ny), (dz, tz, nz)):
                    if step:
                        ok = (at < size) if step > 0 else (at >= 0)
                        inside = ok if inside is None else inside & ok
                source, target = ends(neg(offset))
                yield inside, pltpu.make_async_remote_copy(
                    src_ref=source,
                    dst_ref=target,
                    send_sem=halo_send.at[e, SLOT[offset]],
                    recv_sem=halo_recv.at[e, SLOT[offset]],
                    device_id=(tx, ty, tz),
                    device_id_type=MESH,
                )

        def begin():
            for inside, copy in copies():
                pl.when(inside)(copy.start)

        def finish():
            for inside, copy in landings():
                pl.when(inside)(copy.wait_recv)
            for inside, copy in copies():
                pl.when(inside)(copy.wait_send)

        return begin, finish

    def tensor_ends(offset):
        dx, dy, dz = offset
        if dz:
            return t_zpack, t_zr.at[ZINDEX[neg(offset)]]
        if dx and dy:
            return t_ypack.at[(dy + 1) // 2, 0], t_xyr.at[XYINDEX[neg(offset)]]
        if dx:
            source, target = (bx, 0) if dx > 0 else (1, bx + 1)
            return tens.at[pl.ds(0, 3), source, pl.ds(TOP, by)], tens.at[
                pl.ds(0, 3), target, pl.ds(TOP, by)
            ]
        return t_ypack.at[(dy + 1) // 2], t_yr.at[(1 - dy) // 2]

    def field_ends(e):
        def ends(offset):
            dx, dy, dz = offset
            if dz:
                return f_zpack.at[e], f_zr.at[e, ZINDEX[neg(offset)]]
            if dx and dy:
                return f_ypack.at[e, (dy + 1) // 2], f_xyr.at[e, XYINDEX[neg(offset)]]
            if dx:
                source, target = (bx, 0) if dx > 0 else (1, bx + 1)
                return field.at[e, source, pl.ds(TOP, by)], field.at[e, target, pl.ds(TOP, by)]
            return f_ypack.at[e, (dy + 1) // 2], f_yr.at[e, (1 - dy) // 2]

        return ends

    spread(msg1, gat1, 0)
    begin, finish = exchange(0, tensor_ends)
    begin()
    finish()

    def corners_in(buffer, arrived):
        for offset in XYOFFSETS:
            dx, dy, _ = offset
            x = bx + 1 if dx > 0 else 0
            y = TOP + by if dy > 0 else TOP - 1
            row = 0 if dx > 0 else hi_x
            buffer[x, y : y + 1, :] = arrived[XYINDEX[offset], row : row + 1, :]

    def lines_in(buffer, arrived, side):
        y = TOP - 1 if side == 0 else TOP + by
        for x in range(bx):
            buffer[1 + x, y : y + 1, :] = arrived[x : x + 1, :]

    def shifted(cells, dz, column):
        turned = pltpu.roll(cells, bz - 1 if dz > 0 else 1, 1)
        edge = bz - 1 if dz > 0 else 0
        return jnp.where(iota(cells.shape, 1) == edge, column, turned)

    def tilt(centre, up, down, arrived, i, lines, with_x, with_y):
        stack = []
        for dz in (1, -1):
            r = i if dz > 0 else i + 3

            def row_of(offset):
                return arrived[ZINDEX[offset], r : r + 1, :]

            stack.append(row_of((0, 0, dz)))
            stack.append(
                jnp.where(lane1 < by, row_of((1, 0, dz)), row_of((-1, 0, dz)))
                if with_x
                else jnp.zeros((1, bz), F32)
            )
            stack.append(
                jnp.where(lane1 % by == 0, row_of((0, 1, dz)), row_of((0, -1, dz)))
                if with_y
                else jnp.zeros((1, bz), F32)
            )
        stack = stack + [jnp.zeros((2, bz), F32)]
        columns = jnp.concatenate(stack, axis=0).T
        cells = centre[own, rows, :].reshape(bx * by, bz)
        for dz, out, k in ((1, up, 0), (-1, down, 3)):
            moved = shifted(cells, dz, columns[:, k : k + 1])
            out[own, rows, :] = moved.reshape(bx, by, bz)
            if with_x:
                out[0, rows, :] = shifted(
                    centre[0, rows, :], dz, columns[hi_x * by : bx * by, k + 1 : k + 2]
                )
                out[bx + 1, rows, :] = shifted(
                    centre[bx + 1, rows, :], dz, columns[0:by, k + 1 : k + 2]
                )
            if with_y:
                for side, at, inner in ((0, TOP - 1, hi_y), (1, TOP + by, 0)):
                    edge = jnp.concatenate(
                        [
                            columns[x * by + inner : x * by + inner + 1, k + 2 : k + 3]
                            for x in range(bx)
                        ],
                        axis=0,
                    )
                    moved = shifted(lines[side], dz, edge)
                    for x in range(bx):
                        out[1 + x, at : at + 1, :] = moved[x : x + 1, :]

    for side in range(2):
        for i, slot in enumerate((XY, YY, YZ)):
            lines_in(tens.at[slot], t_yr.at[side, i], side)
    corners_in(tens.at[XY], t_xyr)
    for slot, with_x, with_y in ((XZ, True, False), (YZ, False, True), (ZZ, False, False)):
        i = ZSLOT[slot]
        tilt(
            tens.at[slot],
            tens_p.at[i],
            tens_m.at[i],
            t_zr,
            i,
            (t_yr[0, 2], t_yr[1, 2]),
            with_x,
            with_y,
        )

    for t, (dx, dy, dz, slot, factor) in enumerate(TAPS):
        for x in range(bx):
            here = tens[slot, 1 + x, rows, :]
            there_rows = slice(TOP + dy, TOP + dy + by)
            if dz:
                beside = tens_p if dz > 0 else tens_m
                there = beside[ZSLOT[slot], 1 + x + dx, there_rows, :]
            else:
                there = tens[slot, 1 + x + dx, there_rows, :]
            weight[t, x] = factor * (here + there)

    gathered(gat1, 0)
    for d in range(count):
        den1[d * zblk : (d + 1) * zblk, :] = gat1[d]
    every = den1[...]
    lane_b = iota(every.shape, 1)
    number = every[:, COARSE + 2 : COARSE + 3]
    hot = (lane_b.astype(F32) == number).astype(F32)
    rhs = jnp.sum(every[:, COARSE + 1 : COARSE + 2] * hot, axis=0, keepdims=True)
    parts = jnp.where(lane_b <= COARSE, every, 0.0)
    flow = lax.dot_general(
        hot, parts, (((0,), (0,)), ((), ())), precision=HIGHEST, preferred_element_type=F32
    )
    back = lax.dot_general(
        parts, hot, (((0,), (0,)), ((), ())), precision=HIGHEST, preferred_element_type=F32
    )
    flow, back = flow[0:COARSE], back[0:COARSE]
    row_c, lane_c = iota((COARSE, LANES), 0), iota((COARSE, LANES), 1)
    outward = jnp.sum(flow, axis=1, keepdims=True)
    inward = jnp.sum(flow, axis=0, keepdims=True)
    coarse = jnp.where(row_c == lane_c, outward + inward, 0.0) - flow - back
    work = jnp.where(
        lane_c < COARSE,
        (row_c == lane_c).astype(F32),
        pltpu.roll(jnp.where(lane_c < COARSE, coarse, 0.0), COARSE, 1),
    )
    for k in range(COARSE):
        column = jnp.broadcast_to(work[:, COARSE + k : COARSE + k + 1], (COARSE, LANES))
        row = work[k : k + 1, :] / column[k : k + 1, :]
        work = jnp.where(row_c == k, row, work - column * row)
    inverse[0:COARSE, :] = jnp.where(lane_c < COARSE, work, 0.0)
    inverse[COARSE:LANES, :] = jnp.zeros((LANES - COARSE, LANES), F32)

    def solve(row):
        wide = jnp.broadcast_to(row, (8, LANES))
        got = jnp.dot(wide, inverse[...], precision=HIGHEST, preferred_element_type=F32)
        return got[0:1]

    row16, lane16 = iota((16, LANES), 0), iota((16, LANES), 1)
    place16, block16 = lane16 % span, lane16 // span

    def steps(values):
        flat_rows = jnp.zeros((16, LANES), F32)
        up_rows, down_rows = flat_rows, flat_rows
        for j in range(zblk):
            u = jnp.sum(around[j] * values, axis=1, keepdims=True)
            mine = block16 == j
            flat_rows = jnp.where(mine, u[16:32], flat_rows)
            up_rows = jnp.where(mine, jnp.where(place16 == span - 1, u[32:48], u[16:32]), up_rows)
            down_rows = jnp.where(mine, jnp.where(place16 == 0, u[0:16], u[16:32]), down_rows)
        centre = flat_rows[4:5]
        return centre, {0: centre - flat_rows, 1: centre - up_rows, -1: centre - down_rows}

    plane_row = iota((by, bz), 0)

    def coarse_image(diffs, x):
        total = jnp.zeros((by, bz), F32)
        for t, (dx, dy, dz, _, _) in enumerate(TAPS):
            ax = 1 if x + dx >= bx else (-1 if x + dx < 0 else 0)

            def line(ay):
                r = (ax + 1) * 3 + ay + 1
                return diffs[dz][r : r + 1]

            if dz == 0 and ax == 0 and dy == 0:
                continue
            if dy == 0:
                delta = jnp.broadcast_to(line(0), (by, bz))
            else:
                delta = jnp.where(
                    plane_row == (hi_y if dy > 0 else 0), line(dy), line(0)
                )
            total = total + weight[t, x] * delta
        return total

    def begin_field(e):
        cells = field[e, own, rows, :]
        f_zpack[e] = faces(cells, 0)
        for side, y in ((0, 0), (1, hi_y)):
            for x in range(bx):
                f_ypack[e, side, x : x + 1, :] = field[e, 1 + x, TOP + y : TOP + y + 1, :]
        begin, finish = exchange(1 + e, field_ends(e))
        begin()
        return finish

    def operate(e):
        base = field.at[e]
        for side in range(2):
            lines_in(base, f_yr.at[e, side], side)
        corners_in(base, f_xyr.at[e])
        tilt(
            base, field_p, field_m, f_zr.at[e], 0, (f_yr[e, 0], f_yr[e, 1]), True, True
        )
        norm = jnp.zeros((by, bz), F32)
        cross, total = norm, norm
        for x in range(bx):
            here = base[1 + x, rows, :]
            acc = jnp.zeros((by, bz), F32)
            for t, (dx, dy, dz, _, _) in enumerate(TAPS):
                source = base if dz == 0 else (field_p if dz > 0 else field_m)
                there = source[1 + x + dx, TOP + dy : TOP + dy + by, :]
                acc = acc + weight[t, x] * (here - there)
            prod[x] = acc
            norm = norm + here * here
            cross = cross + here * acc
            total = total + acc
        sums = halves(jnp.sum(total, axis=0, keepdims=True))
        row = jnp.zeros((1, LANES), F32)
        for j in range(zblk):
            row = row + jnp.where(lane1 == own_id[j], sums[j], 0.0)
        row = jnp.where(lane1 == COARSE, jnp.sum(norm), row)
        row = jnp.where(lane1 == COARSE + 1, jnp.sum(cross), row)
        msg2[e] = row
        gat2[e, me] = row
        spread(msg2.at[e], gat2.at[e], 1 + e)

    def collect(e):
        gathered(gat2.at[e], 1 + e)
        for d in range(count):
            den2[d : d + 1, :] = gat2[e, d]
        row = jnp.sum(den2[...], axis=0, keepdims=True)
        values = solve(row)
        shared = jnp.sum(row * values, axis=1, keepdims=True)
        norm = row[:, COARSE : COARSE + 1]
        cross = row[:, COARSE + 1 : COARSE + 2] - shared
        return values, norm, cross

    values0 = solve(rhs)
    centre0, diffs = steps(values0)
    for x in range(bx):
        field[0, 1 + x, rows, :] = right_ref[x] - coarse_image(diffs, x)
    finish = begin_field(0)
    finish()
    operate(0)
    values1, norm0, curve0 = collect(0)
    centre1, diffs = steps(values1)
    alpha0 = norm0 / curve0
    for x in range(bx):
        moved = prod[x] - coarse_image(diffs, x)
        image[x] = moved
        field[1, 1 + x, rows, :] = field[0, 1 + x, rows, :] - alpha0 * moved
    finish = begin_field(1)
    finish()
    operate(1)
    values2, norm1, curve1 = collect(1)
    centre2, diffs = steps(values2)
    beta = norm1 / norm0
    alpha1 = norm1 / (curve1 - beta * norm1 / alpha0)
    both = alpha0 + alpha1 * beta
    coarse_row = centre0 - both * centre1 - alpha1 * centre2
    for x in range(bx):
        moved = prod[x] - coarse_image(diffs, x) + beta * image[x]
        now = field[1, 1 + x, rows, :]
        res_ref[x] = now - alpha1 * moved
        sol_ref[x] = coarse_row + both * field[0, 1 + x, rows, :] + alpha1 * now


def solution(mesh):
    nx, ny, nz = (mesh.shape[name] for name in ("gx", "gy", "gz"))
    count = nx * ny * nz

    def body(right_side, fiber_class, conductivity_scale, class_tensor, block_ids):
        bx, by, bz = right_side.shape
        nbx, nby, nbz = block_ids.shape
        zblk = nbz // nz
        dims = (nx, ny, nz, bx, by, zblk, nbx, nby, nbz)
        px, py = bx + 2, by + 16
        vmem = lambda *shape: pltpu.VMEM(shape, F32)
        whole = pl.BlockSpec(memory_space=pltpu.VMEM)
        scalar = pl.BlockSpec(memory_space=pltpu.SMEM)
        return pl.pallas_call(
            functools.partial(kernel, dims),
            out_shape=[jax.ShapeDtypeStruct((bx, by, bz), F32)] * 2,
            in_specs=[scalar, scalar, whole, whole, whole],
            out_specs=[whole, whole],
            scratch_shapes=[
                vmem(6, px, py, bz),
                vmem(3, px, py, bz),
                vmem(3, px, py, bz),
                vmem(18, bx, by, bz),
                vmem(2, px, py, bz),
                vmem(px, py, bz),
                vmem(px, py, bz),
                vmem(bx, by, bz),
                vmem(bx, by, bz),
                vmem(48, bz),
                vmem(LANES, LANES),
                vmem(2, 3, bx, bz),
                vmem(2, 3, bx, bz),
                vmem(4, bx, bz),
                vmem(8, bz),
                vmem(len(ZOFFSETS), 8, bz),
                vmem(2, 2, bx, bz),
                vmem(2, 2, bx, bz),
                vmem(2, 4, bx, bz),
                vmem(2, 8, bz),
                vmem(2, len(ZOFFSETS), 8, bz),
                vmem(zblk, LANES),
                vmem(count, zblk, LANES),
                vmem(count * zblk, LANES),
                vmem(2, 1, LANES),
                vmem(2, count, 1, LANES),
                vmem(count, LANES),
                pltpu.SemaphoreType.DMA((3, 18)),
                pltpu.SemaphoreType.DMA((3, 18)),
                pltpu.SemaphoreType.DMA((3,)),
                pltpu.SemaphoreType.DMA((3,)),
            ],
            compiler_params=pltpu.CompilerParams(collective_id=0, has_side_effects=True),
        )(block_ids, class_tensor, right_side, fiber_class, conductivity_scale)

    placed = (P("gx", "gy", "gz"), P("gx", "gy", "gz"), P("gx", "gy", "gz"), P(), P())
    return jax.shard_map(
        body,
        mesh=mesh,
        in_specs=placed,
        out_specs=(P("gx", "gy", "gz"), P("gx", "gy", "gz")),
        check_vma=False,
    )
```

time: 367 us -> 40.8 us (0.11)
  blocking collectives: 179 us -> 0 us
  starting transfers between devices: 112 us -> 0 us
  Pallas kernels: 0 us -> 37.9 us
  waiting for transfers between devices: 25.1 us -> 0 us
  other arithmetic: 22.3 us -> 0 us
  matrix products: 13.4 us -> 0 us
  between operations: 8.31 us -> 0.65 us
    psum x4 -> x0, blocking collectives: 179 us -> none  [the longest x2 97.5 us: joint_terms(): lax.psum((restrict(product), jnp.sum(field * field), jnp.sum(field * prod...]
    ppermute x42 -> x0, starting transfers between devices: 112 us -> none  [the longest x21 84.8 us: padded_2(): lax.ppermute(tail, axis, [(i, (i + 1) % count) for i in range(ends)])]
    pallas_call x0 -> x1, Pallas kernels: none -> 37.9 us  [body(): pl.pallas_call(functools.partial(kernel, dims), out_shape=[jax.ShapeDtype...]
    ppermute x42 -> x0, waiting for transfers between devices: 25.1 us -> none  [the longest x21 14.1 us: padded_2(): lax.ppermute(tail, axis, [(i, (i + 1) % count) for i in range(ends)])]
    another operation x6 -> x0, other arithmetic: 12.1 us -> none  [the longest x3 6.52 us: body(): factor_lower = jnp.linalg.cholesky(coarse)]
    dot_general x65 -> x0, matrix products: 10.9 us -> none  [the longest x54 8.59 us: body(): jnp.einsum('xyz,xa,yb,zjc->jabc', weight, reach_onehot(CX, step_x), reach...]
    reduce_sum x9 -> x0, other arithmetic: 4.12 us -> none  [the longest x1 1.65 us: build_tensors(): jnp.sum(jnp.where(matches, class_tensor[component][:, None, None, None],...]
  transfers between devices with their start and end apart: 42 -> 0, of which waited for: 16 -> 0; matrix products, arithmetic and copies ran while one was open for 1% -> 0% of each run, Pallas kernels for 0% -> 0%
where the time goes in v1:
time: 40.8 us; the launch traced here: 40.6 us
  Pallas kernels  37.9 us (93%)
  local copies, waits for them, and re-layouts  2.14 us (5%)
  between operations  0.65 us (2%)
    pallas_call x1, Pallas kernels, body(): pl.pallas_call(functools.partial(kernel, dims), out_shape=[jax.ShapeDtype...  37.9 us
    unnamed x4, local copies, waits for them, and re-layouts  2.14 us

profile of v1, /device:TPU:0, one launch (start us, length us, event | category | flops | bytes accessed | tf_op | source)
XLA Modules:
  0.0 40.6 jit_solution(2138998286718850295)
XLA Ops:
  0.6 37.9 %shard_map.68 = (f32[8,16,128]{2,1,0:T(8,128)}, f32[8,16,128]{2,1,0:T(8,128)}) custom-call(s32[2,4,8]{2,1,0:T(4,128)} %ids_ref.1, f32[6,16]{1,0:T(8,128)} %table_ref.1, f32[8,16,128]{2,1,0:T(8,128)} %right_ref.1, s32[8,16,128]{2,1,0:T(8,128)} %class_ref.1, f32[8,16,128]{2,1,0:T(8,128)} %scale_ref.1), custom_call_target="tpu_custom_call" | custom-call | tf_op jit(solution)/shard_map/pallas_call | solution.py:624
  38.5 0.0 copy-start
  38.5 1.5 %copy.9 = f32[8,16,128]{2,1,0:T(8,128)} copy(f32[8,16,128]{2,1,0:T(8,128)} %get-tuple-element.4) | data formatting | bytes 131072
  40.0 0.0 copy-done
  40.0 0.6 %copy.10 = f32[8,16,128]{2,1,0:T(8,128)} copy(f32[8,16,128]{2,1,0:T(8,128)S(1)} %copy-done) | data formatting | bytes 131072
Async XLA Ops:
  38.5 1.5 %copy-start = (f32[8,16,128]{2,1,0:T(8,128)S(1)}, f32[8,16,128]{2,1,0:T(8,128)}, u32[]{:S(2)}) copy-start(f32[8,16,128]{2,1,0:T(8,128)} %get-tuple-element.5) | copy-start | bytes 196612

commit v2 on v1

--- a/solution.py
+++ b/solution.py
@@ -8,6 +8,7 @@
 from jax.sharding import PartitionSpec as P
 
 COARSE = 64
+PIVOTS = 4
 LANES = 128
 HIGHEST = lax.Precision.HIGHEST
 MESH = pl.DeviceIdType.MESH
@@ -89,7 +90,6 @@
     den1,
     msg2,
     gat2,
-    den2,
     halo_send,
     halo_recv,
     gat_send,
@@ -116,11 +116,37 @@
         t = lax.rem(me + d, count)
         return (lax.div(t, ny * nz), lax.rem(lax.div(t, nz), ny), lax.rem(t, nz))
 
+    steps_far = sorted(
+        (
+            (dx, dy, dz)
+            for dx in range(nx)
+            for dy in range(ny)
+            for dz in range(nz)
+            if dx or dy or dz
+        ),
+        key=lambda o: -sum(min(d, n - d) for d, n in zip(o, (nx, ny, nz // 2))),
+    )
+
+    def each_peer(action):
+        if count > 64:
+            pl.loop(1, count)(lambda d: action(other(d)))
+            return
+
+        def turned(at, n):
+            return [at] + [
+                jnp.where(at + d >= n, at + d - n, at + d) for d in range(1, n)
+            ]
+
+        xs, ys, zs = turned(px, nx), turned(py, ny), turned(pz, nz)
+        for dx, dy, dz in steps_far:
+            action((xs[dx], ys[dy], zs[dz]))
+
     barrier = pltpu.get_barrier_semaphore()
 
-    @pl.loop(1, count)
-    def _(d):
-        pl.semaphore_signal(barrier, inc=1, device_id=other(d), device_id_type=MESH)
+    def greet(peer):
+        pl.semaphore_signal(barrier, inc=1, device_id=peer, device_id_type=MESH)
+
+    each_peer(greet)
 
     lane1 = iota((1, bz), 1)
     place = lane1 % span
@@ -254,17 +280,20 @@
 
     pl.semaphore_wait(barrier, count - 1)
 
+    later = []
+
     def spread(msg, gat, g):
-        @pl.loop(1, count)
-        def _(d):
+        def send(peer):
             pltpu.make_async_remote_copy(
                 src_ref=msg,
                 dst_ref=gat.at[me],
                 send_sem=gat_send.at[g],
                 recv_sem=gat_recv.at[g],
-                device_id=other(d),
+                device_id=peer,
                 device_id_type=MESH,
             ).start()
+
+        each_peer(send)
 
     def gathered(gat, g):
         every = pltpu.make_async_remote_copy(
@@ -275,8 +304,8 @@
             device_id=other(1),
             device_id_type=MESH,
         )
-        every.wait_send()
         every.wait_recv()
+        later.append(every.wait_send)
 
     def exchange(e, ends):
         def copies():
@@ -325,7 +354,7 @@
             for inside, copy in landings():
                 pl.when(inside)(copy.wait_recv)
             for inside, copy in copies():
-                pl.when(inside)(copy.wait_send)
+                later.append(functools.partial(pl.when(inside), copy.wait_send))
 
         return begin, finish
 
@@ -441,16 +470,16 @@
             with_y,
         )
 
-    for t, (dx, dy, dz, slot, factor) in enumerate(TAPS):
-        for x in range(bx):
-            here = tens[slot, 1 + x, rows, :]
-            there_rows = slice(TOP + dy, TOP + dy + by)
-            if dz:
-                beside = tens_p if dz > 0 else tens_m
-                there = beside[ZSLOT[slot], 1 + x + dx, there_rows, :]
-            else:
-                there = tens[slot, 1 + x + dx, there_rows, :]
-            weight[t, x] = factor * (here + there)
+    def weigh(t, x):
+        dx, dy, dz, slot, factor = TAPS[t]
+        here = tens[slot, 1 + x, rows, :]
+        there_rows = slice(TOP + dy, TOP + dy + by)
+        if dz:
+            beside = tens_p if dz > 0 else tens_m
+            there = beside[ZSLOT[slot], 1 + x + dx, there_rows, :]
+        else:
+            there = tens[slot, 1 + x + dx, there_rows, :]
+        weight[t, x] = factor * (here + there)
 
     gathered(gat1, 0)
     for d in range(count):
@@ -477,12 +506,42 @@
         (row_c == lane_c).astype(F32),
         pltpu.roll(jnp.where(lane_c < COARSE, coarse, 0.0), COARSE, 1),
     )
-    for k in range(COARSE):
-        column = jnp.broadcast_to(work[:, COARSE + k : COARSE + k + 1], (COARSE, LANES))
-        row = work[k : k + 1, :] / column[k : k + 1, :]
-        work = jnp.where(row_c == k, row, work - column * row)
+    units = [(t, x) for x in range(bx) for t in range(len(TAPS))]
+    share = -(-len(units) * PIVOTS // COARSE)
+    for k in range(0, COARSE, PIVOTS):
+        columns = [
+            jnp.broadcast_to(work[:, COARSE + k + c : COARSE + k + c + 1], (COARSE, LANES))
+            for c in range(PIVOTS)
+        ]
+        lines = [work[k + i : k + i + 1, :] for i in range(PIVOTS)]
+        pivot = [[columns[c][k + i : k + i + 1, :] for c in range(PIVOTS)] for i in range(PIVOTS)]
+        for unit in units[:share]:
+            weigh(*unit)
+        units = units[share:]
+        for i in range(PIVOTS):
+            scale = 1.0 / pivot[i][i]
+            lines[i] = lines[i] * scale
+            for c in range(i + 1, PIVOTS):
+                pivot[i][c] = pivot[i][c] * scale
+            for r in range(PIVOTS):
+                if r != i:
+                    ratio = pivot[r][i]
+                    lines[r] = lines[r] - ratio * lines[i]
+                    for c in range(i + 1, PIVOTS):
+                        pivot[r][c] = pivot[r][c] - ratio * pivot[i][c]
+        for c in range(PIVOTS):
+            work = work - columns[c] * lines[c]
+        for i in range(PIVOTS):
+            work = jnp.where(row_c == k + i, lines[i], work)
+    for unit in units:
+        weigh(*unit)
     inverse[0:COARSE, :] = jnp.where(lane_c < COARSE, work, 0.0)
     inverse[COARSE:LANES, :] = jnp.zeros((LANES - COARSE, LANES), F32)
+
+    reach = [
+        jnp.dot(near, inverse[...], precision=HIGHEST, preferred_element_type=F32)
+        for near in around
+    ]
 
     def solve(row):
         wide = jnp.broadcast_to(row, (8, LANES))
@@ -492,11 +551,11 @@
     row16, lane16 = iota((16, LANES), 0), iota((16, LANES), 1)
     place16, block16 = lane16 % span, lane16 // span
 
-    def steps(values):
+    def steps(row):
         flat_rows = jnp.zeros((16, LANES), F32)
         up_rows, down_rows = flat_rows, flat_rows
         for j in range(zblk):
-            u = jnp.sum(around[j] * values, axis=1, keepdims=True)
+            u = jnp.sum(reach[j] * row, axis=1, keepdims=True)
             mine = block16 == j
             flat_rows = jnp.where(mine, u[16:32], flat_rows)
             up_rows = jnp.where(mine, jnp.where(place16 == span - 1, u[32:48], u[16:32]), up_rows)
@@ -526,9 +585,14 @@
             total = total + weight[t, x] * delta
         return total
 
+    index_f = iota((bx * by, LANES), 0)
+    same_f = index_f == iota((bx * by, LANES), 1)
+
     def begin_field(e):
-        cells = field[e, own, rows, :]
-        f_zpack[e] = faces(cells, 0)
+        cells = field[e, own, rows, :].reshape(bx * by, bz)
+        for r, at in ((0, 0), (3, bz - 1)):
+            column = jnp.where(same_f, cells[:, at : at + 1], 0.0)
+            f_zpack[e, r : r + 1, :] = jnp.sum(column, axis=0, keepdims=True)
         for side, y in ((0, 0), (1, hi_y)):
             for x in range(bx):
                 f_ypack[e, side, x : x + 1, :] = field[e, 1 + x, TOP + y : TOP + y + 1, :]
@@ -557,36 +621,38 @@
             norm = norm + here * here
             cross = cross + here * acc
             total = total + acc
-        sums = halves(jnp.sum(total, axis=0, keepdims=True))
+        total = jnp.sum(total, axis=0, keepdims=True)
+        lists = [jnp.where(block == j, total, 0.0) for j in range(zblk)]
+        lists += [jnp.sum(norm, axis=0, keepdims=True), jnp.sum(cross, axis=0, keepdims=True)]
+        sums = jnp.sum(jnp.concatenate(lists, axis=0), axis=1, keepdims=True)
         row = jnp.zeros((1, LANES), F32)
-        for j in range(zblk):
-            row = row + jnp.where(lane1 == own_id[j], sums[j], 0.0)
-        row = jnp.where(lane1 == COARSE, jnp.sum(norm), row)
-        row = jnp.where(lane1 == COARSE + 1, jnp.sum(cross), row)
+        for i, at in enumerate(own_id + [COARSE, COARSE + 1]):
+            row = row + jnp.where(lane1 == at, sums[i : i + 1], 0.0)
         msg2[e] = row
         gat2[e, me] = row
         spread(msg2.at[e], gat2.at[e], 1 + e)
 
     def collect(e):
         gathered(gat2.at[e], 1 + e)
-        for d in range(count):
-            den2[d : d + 1, :] = gat2[e, d]
-        row = jnp.sum(den2[...], axis=0, keepdims=True)
+        terms = [gat2[e, d] for d in range(count)]
+        while len(terms) > 1:
+            pairs = [a + b for a, b in zip(terms[0::2], terms[1::2])]
+            terms = pairs + terms[len(pairs) * 2 :]
+        row = terms[0]
         values = solve(row)
         shared = jnp.sum(row * values, axis=1, keepdims=True)
         norm = row[:, COARSE : COARSE + 1]
         cross = row[:, COARSE + 1 : COARSE + 2] - shared
-        return values, norm, cross
-
-    values0 = solve(rhs)
-    centre0, diffs = steps(values0)
+        return row, norm, cross
+
+    centre0, diffs = steps(rhs)
     for x in range(bx):
         field[0, 1 + x, rows, :] = right_ref[x] - coarse_image(diffs, x)
     finish = begin_field(0)
     finish()
     operate(0)
-    values1, norm0, curve0 = collect(0)
-    centre1, diffs = steps(values1)
+    row0, norm0, curve0 = collect(0)
+    centre1, diffs = steps(row0)
     alpha0 = norm0 / curve0
     for x in range(bx):
         moved = prod[x] - coarse_image(diffs, x)
@@ -595,8 +661,8 @@
     finish = begin_field(1)
     finish()
     operate(1)
-    values2, norm1, curve1 = collect(1)
-    centre2, diffs = steps(values2)
+    row1, norm1, curve1 = collect(1)
+    centre2, diffs = steps(row1)
     beta = norm1 / norm0
     alpha1 = norm1 / (curve1 - beta * norm1 / alpha0)
     both = alpha0 + alpha1 * beta
@@ -606,6 +672,8 @@
         now = field[1, 1 + x, rows, :]
         res_ref[x] = now - alpha1 * moved
         sol_ref[x] = coarse_row + both * field[0, 1 + x, rows, :] + alpha1 * now
+    for wait in later:
+        wait()
 
 
 def solution(mesh):
@@ -653,7 +721,6 @@
                 vmem(count * zblk, LANES),
                 vmem(2, 1, LANES),
                 vmem(2, count, 1, LANES),
-                vmem(count, LANES),
                 pltpu.SemaphoreType.DMA((3, 18)),
                 pltpu.SemaphoreType.DMA((3, 18)),
                 pltpu.SemaphoreType.DMA((3,)),

time: 40.8 us -> 36.9 us (0.904)
  Pallas kernels: 37.9 us -> 33.9 us
    pallas_call x1, Pallas kernels: 37.9 us -> 33.9 us  [body(): pl.pallas_call(functools.partial(kernel, dims), out_shape=[jax.ShapeDtype...]
where the time goes in v2:
time: 36.9 us; the launch traced here: 36.6 us
  Pallas kernels  33.9 us (92%)
  local copies, waits for them, and re-layouts  2.14 us (6%)
  between operations  0.65 us (2%)
    pallas_call x1, Pallas kernels, body(): pl.pallas_call(functools.partial(kernel, dims), out_shape=[jax.ShapeDtype...  33.9 us
    unnamed x4, local copies, waits for them, and re-layouts  2.14 us

profile of v2, /device:TPU:0, one launch (start us, length us, event | category | flops | bytes accessed | tf_op | source)
XLA Modules:
  0.0 36.6 jit_solution(13959783859498100830)
XLA Ops:
  0.6 33.9 %shard_map.68 = (f32[8,16,128]{2,1,0:T(8,128)}, f32[8,16,128]{2,1,0:T(8,128)}) custom-call(s32[2,4,8]{2,1,0:T(4,128)} %ids_ref.1, f32[6,16]{1,0:T(8,128)} %table_ref.1, f32[8,16,128]{2,1,0:T(8,128)} %right_ref.1, s32[8,16,128]{2,1,0:T(8,128)} %class_ref.1, f32[8,16,128]{2,1,0:T(8,128)} %scale_ref.1), custom_call_target="tpu_custom_call" | custom-call | tf_op jit(solution)/shard_map/pallas_call | solution.py:692
  34.5 0.0 copy-start
  34.5 1.5 %copy.9 = f32[8,16,128]{2,1,0:T(8,128)} copy(f32[8,16,128]{2,1,0:T(8,128)} %get-tuple-element.4) | data formatting | bytes 131072
  36.0 0.0 copy-done
  36.0 0.6 %copy.10 = f32[8,16,128]{2,1,0:T(8,128)} copy(f32[8,16,128]{2,1,0:T(8,128)S(1)} %copy-done) | data formatting | bytes 131072
Async XLA Ops:
  34.5 1.5 %copy-start = (f32[8,16,128]{2,1,0:T(8,128)S(1)}, f32[8,16,128]{2,1,0:T(8,128)}, u32[]{:S(2)}) copy-start(f32[8,16,128]{2,1,0:T(8,128)} %get-tuple-element.5) | copy-start | bytes 196612

commit v3 on v2

--- a/solution.py
+++ b/solution.py
@@ -39,6 +39,7 @@
     (0, -1, 1, YZ, -0.25),
 )
 OFFSETS = tuple(tap[:3] for tap in TAPS)
+FAR_FIRST = OFFSETS[6:] + OFFSETS[:6]
 SLOT = {offset: i for i, offset in enumerate(OFFSETS)}
 ZOFFSETS = tuple(o for o in OFFSETS if o[2])
 ZINDEX = {offset: i for i, offset in enumerate(ZOFFSETS)}
@@ -309,7 +310,7 @@
 
     def exchange(e, ends):
         def copies():
-            for offset in OFFSETS:
+            for offset in FAR_FIRST:
                 dx, dy, dz = offset
                 tx, ty, tz = px + dx, py + dy, pz + dz
                 inside = None
@@ -328,7 +329,7 @@
                 )
 
         def landings():
-            for offset in OFFSETS:
+            for offset in FAR_FIRST:
                 dx, dy, dz = offset
                 tx, ty, tz = px + dx, py + dy, pz + dz
                 inside = None
@@ -726,7 +727,9 @@
                 pltpu.SemaphoreType.DMA((3,)),
                 pltpu.SemaphoreType.DMA((3,)),
             ],
-            compiler_params=pltpu.CompilerParams(collective_id=0, has_side_effects=True),
+            compiler_params=pltpu.CompilerParams(
+                collective_id=0, has_side_effects=True, vmem_limit_bytes=16 * 1024 * 1024
+            ),
         )(block_ids, class_tensor, right_side, fiber_class, conductivity_scale)
 
     placed = (P("gx", "gy", "gz"), P("gx", "gy", "gz"), P("gx", "gy", "gz"), P(), P())

time: 36.9 us -> 39.1 us (1.060)
  local copies, waits for them, and re-layouts: 2.14 us -> 5.14 us
  Pallas kernels: 33.9 us -> 32.9 us
    unnamed x4 -> x12, local copies, waits for them, and re-layouts: 2.14 us -> 5.14 us
    pallas_call x1, Pallas kernels: 33.9 us -> 32.9 us  [body(): pl.pallas_call(functools.partial(kernel, dims), out_shape=[jax.ShapeDtype...]
where the time goes in v3:
time: 39.1 us; the launch traced here: 38.7 us
  Pallas kernels  32.9 us (84%)
  local copies, waits for them, and re-layouts  5.14 us (13%)
  between operations  0.65 us (2%)
    pallas_call x1, Pallas kernels, body(): pl.pallas_call(functools.partial(kernel, dims), out_shape=[jax.ShapeDtype...  32.9 us
    unnamed x12, local copies, waits for them, and re-layouts  5.14 us

profile of v3, /device:TPU:0, one launch (start us, length us, event | category | flops | bytes accessed | tf_op | source)
XLA Modules:
  0.0 38.7 jit_solution(6655582444683535320)
XLA Ops:
  0.6 0.0 copy-start
  0.6 0.8 %copy-done = f32[8,16,128]{2,1,0:T(8,128)S(1)} copy-done((f32[8,16,128]{2,1,0:T(8,128)S(1)}, f32[8,16,128]{2,1,0:T(8,128)}, u32[]{:S(2)}) %copy-start) | copy-done | bytes 65560
  1.5 0.0 copy-start.1
  1.5 0.8 %copy-done.1 = s32[8,16,128]{2,1,0:T(8,128)S(1)} copy-done((s32[8,16,128]{2,1,0:T(8,128)S(1)}, s32[8,16,128]{2,1,0:T(8,128)}, u32[]{:S(2)}) %copy-start.1) | copy-done | bytes 65560
  2.3 0.0 copy-start.2
  2.3 0.8 %copy-done.2 = f32[8,16,128]{2,1,0:T(8,128)S(1)} copy-done((f32[8,16,128]{2,1,0:T(8,128)S(1)}, f32[8,16,128]{2,1,0:T(8,128)}, u32[]{:S(2)}) %copy-start.2) | copy-done | bytes 65560
  3.2 0.0 copy-start.3
  3.2 0.7 %copy-done.3 = s32[2,4,8]{2,1,0:T(4,128)S(1)} copy-done((s32[2,4,8]{2,1,0:T(4,128)S(1)}, s32[2,4,8]{2,1,0:T(4,128)}, u32[]{:S(2)}) %copy-start.3) | copy-done | bytes 280
  3.8 0.0 copy-start.4
  3.8 0.7 %copy-done.4 = f32[6,16]{1,0:T(8,128)S(1)} copy-done((f32[6,16]{1,0:T(8,128)S(1)}, f32[6,16]{1,0:T(8,128)}, u32[]{:S(2)}) %copy-start.4) | copy-done | bytes 408
  4.5 32.9 %shard_map.68 = (f32[8,16,128]{2,1,0:T(8,128)S(1)}, f32[8,16,128]{2,1,0:T(8,128)S(1)}) custom-call(s32[2,4,8]{2,1,0:T(4,128)S(1)} %copy-done.3, f32[6,16]{1,0:T(8,128)S(1)} %copy-done.4, f32[8,16,128]{2,1,0:T(8,128)S(1)} %copy-done, s32[8,16,128]{2,1,0:T(8,128)S(1)} %copy-done.1, f32[8,16,128]{2,1,0:T(8,128)S(1)} %copy-done.2), custom_call_target="tpu_custom_call" | custom-call | tf_op jit(solution)/shard_map/pallas_call | solution.py:693
  37.5 0.6 %copy.9 = f32[8,16,128]{2,1,0:T(8,128)} copy(f32[8,16,128]{2,1,0:T(8,128)S(1)} %get-tuple-element.4) | data formatting | bytes 131072
  38.1 0.6 %copy.10 = f32[8,16,128]{2,1,0:T(8,128)} copy(f32[8,16,128]{2,1,0:T(8,128)S(1)} %get-tuple-element.5) | data formatting | bytes 131072
Async XLA Ops:
  0.6 0.8 %copy-start = (f32[8,16,128]{2,1,0:T(8,128)S(1)}, f32[8,16,128]{2,1,0:T(8,128)}, u32[]{:S(2)}) copy-start(f32[8,16,128]{2,1,0:T(8,128)} %right_ref.1) | copy-start | bytes 196612
  1.5 0.8 %copy-start.1 = (s32[8,16,128]{2,1,0:T(8,128)S(1)}, s32[8,16,128]{2,1,0:T(8,128)}, u32[]{:S(2)}) copy-start(s32[8,16,128]{2,1,0:T(8,128)} %class_ref.1) | copy-start | bytes 196612
  2.3 0.8 %copy-start.2 = (f32[8,16,128]{2,1,0:T(8,128)S(1)}, f32[8,16,128]{2,1,0:T(8,128)}, u32[]{:S(2)}) copy-start(f32[8,16,128]{2,1,0:T(8,128)} %scale_ref.1) | copy-start | bytes 196612
  3.2 0.7 %copy-start.3 = (s32[2,4,8]{2,1,0:T(4,128)S(1)}, s32[2,4,8]{2,1,0:T(4,128)}, u32[]{:S(2)}) copy-start(s32[2,4,8]{2,1,0:T(4,128)} %ids_ref.1) | copy-start | bytes 772
  3.8 0.7 %copy-start.4 = (f32[6,16]{1,0:T(8,128)S(1)}, f32[6,16]{1,0:T(8,128)}, u32[]{:S(2)}) copy-start(f32[6,16]{1,0:T(8,128)} %table_ref.1) | copy-start | bytes 1156

commit v4 on v3

--- a/solution.py
+++ b/solution.py
@@ -58,13 +58,19 @@
 
 def kernel(
     dims,
+    ids_in,
+    table_in,
+    right_in,
+    class_in,
+    scale_in,
+    sol_ref,
+    res_ref,
     ids_ref,
     table_ref,
     right_ref,
     class_ref,
     scale_ref,
-    sol_ref,
-    res_ref,
+    load_sem,
     tens,
     tens_p,
     tens_m,
@@ -105,6 +111,21 @@
     rows = slice(TOP, TOP + by)
     own = slice(1, 1 + bx)
 
+    loads = [
+        pltpu.make_async_copy(source, target, load_sem.at[i])
+        for i, (source, target) in enumerate(
+            (
+                (table_in, table_ref),
+                (ids_in, ids_ref),
+                (class_in, class_ref),
+                (scale_in, scale_ref),
+                (right_in, right_ref),
+            )
+        )
+    ]
+    for load in loads:
+        load.start()
+
     tens[0:3, 0, rows, :] = jnp.zeros((3, by, bz), F32)
     tens[0:3, bx + 1, rows, :] = jnp.zeros((3, by, bz), F32)
     for e in range(2):
@@ -148,6 +169,8 @@
         pl.semaphore_signal(barrier, inc=1, device_id=peer, device_id_type=MESH)
 
     each_peer(greet)
+    for load in loads:
+        load.wait()
 
     lane1 = iota((1, bz), 1)
     place = lane1 % span
@@ -689,13 +712,18 @@
         px, py = bx + 2, by + 16
         vmem = lambda *shape: pltpu.VMEM(shape, F32)
         whole = pl.BlockSpec(memory_space=pltpu.VMEM)
-        scalar = pl.BlockSpec(memory_space=pltpu.SMEM)
         return pl.pallas_call(
             functools.partial(kernel, dims),
             out_shape=[jax.ShapeDtypeStruct((bx, by, bz), F32)] * 2,
-            in_specs=[scalar, scalar, whole, whole, whole],
+            in_specs=[pl.BlockSpec(memory_space=pltpu.HBM)] * 5,
             out_specs=[whole, whole],
             scratch_shapes=[
+                pltpu.SMEM(block_ids.shape, jnp.int32),
+                pltpu.SMEM(class_tensor.shape, F32),
+                vmem(bx, by, bz),
+                pltpu.VMEM((bx, by, bz), jnp.int32),
+                vmem(bx, by, bz),
+                pltpu.SemaphoreType.DMA((5,)),
                 vmem(6, px, py, bz),
                 vmem(3, px, py, bz),
                 vmem(3, px, py, bz),
@@ -728,7 +756,7 @@
                 pltpu.SemaphoreType.DMA((3,)),
             ],
             compiler_params=pltpu.CompilerParams(
-                collective_id=0, has_side_effects=True, vmem_limit_bytes=16 * 1024 * 1024
+                collective_id=0, has_side_effects=True
             ),
         )(block_ids, class_tensor, right_side, fiber_class, conductivity_scale)
 

time: 39.1 us -> 36 us (0.921)
  local copies, waits for them, and re-layouts: 5.14 us -> 2.14 us
    unnamed x12 -> x4, local copies, waits for them, and re-layouts: 5.14 us -> 2.14 us
where the time goes in v4:
time: 36 us; the launch traced here: 35.8 us
  Pallas kernels  33 us (92%)
  local copies, waits for them, and re-layouts  2.14 us (6%)
  between operations  0.65 us (2%)
    pallas_call x1, Pallas kernels, body(): pl.pallas_call(functools.partial(kernel, dims), out_shape=[jax.ShapeDtype...  33 us
    unnamed x4, local copies, waits for them, and re-layouts  2.14 us

profile of v4, /device:TPU:0, one launch (start us, length us, event | category | flops | bytes accessed | tf_op | source)
XLA Modules:
  0.0 35.8 jit_solution(15010904851172125790)
XLA Ops:
  0.6 33.0 %shard_map.68 = (f32[8,16,128]{2,1,0:T(8,128)}, f32[8,16,128]{2,1,0:T(8,128)}) custom-call(s32[2,4,8]{2,1,0:T(4,128)} %ids_in.1, f32[6,16]{1,0:T(8,128)} %table_in.1, f32[8,16,128]{2,1,0:T(8,128)} %right_in.1, s32[8,16,128]{2,1,0:T(8,128)} %class_in.1, f32[8,16,128]{2,1,0:T(8,128)} %scale_in.1), custom_call_target="tpu_custom_call" | custom-call | tf_op jit(solution)/shard_map/pallas_call | solution.py:715
  33.6 0.0 copy-start
  33.6 1.5 %copy.9 = f32[8,16,128]{2,1,0:T(8,128)} copy(f32[8,16,128]{2,1,0:T(8,128)} %get-tuple-element.4) | data formatting | bytes 131072
  35.1 0.0 copy-done
  35.1 0.6 %copy.10 = f32[8,16,128]{2,1,0:T(8,128)} copy(f32[8,16,128]{2,1,0:T(8,128)S(1)} %copy-done) | data formatting | bytes 131072
Async XLA Ops:
  33.6 1.5 %copy-start = (f32[8,16,128]{2,1,0:T(8,128)S(1)}, f32[8,16,128]{2,1,0:T(8,128)}, u32[]{:S(2)}) copy-start(f32[8,16,128]{2,1,0:T(8,128)} %get-tuple-element.5) | copy-start | bytes 196612
